TPU v7x, 32 devices: a whole 2x2x4 slice. The times are simulated.
32 devices in a mesh: ba: 4 (over x, core), ma: 4 (over z), row: 2 (over y).
Axes of the slice: x: 2, y: 2, z: 4, core: 2. Of those that a mesh axis runs over, the one named last changes fastest.
Arguments:
- tokens: bfloat16 [8, 256, 4096], P(('ba', 'row'), None, 'ma'), may hold values from -6 to 6
- attn_gain: bfloat16 [4096], P('ma'), may hold values from 0.25 to 1.75
- query_weight: bfloat16 [4096, 4096], P('row', 'ma'), may hold values from -0.046875 to 0.046875
- key_weight: bfloat16 [4096, 4096], P('row', 'ma'), may hold values from -0.046875 to 0.046875
- value_projection_matrix: bfloat16 [4096, 4096], P('row', 'ma'), may hold values from -0.09375 to 0.09375
- attention_output_matrix: bfloat16 [4096, 4096], P('ma', 'row'), may hold values from -0.125 to 0.125
- bucket_bias_matrix: float32 [32, 64], P(None, 'ma'), may hold values from -6 to 215, as said below
- ffn_gain: bfloat16 [4096], P('ma'), may hold values from 0.25 to 1.75
- gate_weight: bfloat16 [4096, 8192], P(None, ('ma', 'row')), may hold values from -0.09375 to 0.09375
- up_weight: bfloat16 [4096, 8192], P(None, ('ma', 'row')), may hold values from -0.09375 to 0.09375
- down_projection_weight: bfloat16 [8192, 4096], P(('ma', 'row')), may hold values from -0.09375 to 0.09375
Outputs:
- encoded: bfloat16 [8, 256, 4096], P(('ba', 'row'), None, 'ma')
Inputs may be any that keep to these rules, and one draw needn't show every extreme that they name: `bucket_bias_matrix`: entries of the relative position table.
All inputs are finite; a program needn't handle non-finite values.
Results may differ from a plain program's by a relative error of at most 0.017.
Values may be sent and summed in bfloat16 or wider, within the bound.
A program may use at most 128 MiB of HBM per device.

v0:
```python
import jax
import jax.numpy as jnp
from jax import lax
from jax.sharding import PartitionSpec as P

bucket_thresholds = (1, 2, 3, 4, 5, 6, 7, 8, 11, 16, 23, 32, 45, 64, 91, 128)
epsilon = 1e-06


def buckets(length):
    places = jnp.arange(length, dtype=jnp.int32)
    offset = places[None, :] - places[:, None]
    distance = jnp.abs(offset)
    backward = jnp.zeros_like(distance)
    for threshold in bucket_thresholds[:15]:
        backward = backward + (distance >= threshold).astype(jnp.int32)
    forward = jnp.full_like(distance, 15)
    for threshold in bucket_thresholds:
        forward = forward + (distance >= threshold).astype(jnp.int32)
    return jnp.where(offset > 0, forward, backward)


def rms_scale(values, gain):
    mean_square = jnp.mean(values * values, axis=-1, keepdims=True)
    return (values * lax.rsqrt(mean_square + epsilon) * gain.astype(jnp.float32)).astype(
        jnp.bfloat16
    )


def regroup(values, norm_gain_vector):
    widened = (
        lax.all_gather(values, "ma", axis=1, tiled=True),
        lax.all_gather(norm_gain_vector, "ma", axis=1, tiled=True),
    )
    stacked = lax.all_gather(widened[0], "row", axis=0, tiled=True)
    return (stacked, widened[1])


def on_device(
    tokens,
    attn_gain,
    query_weight,
    key_weight,
    value_projection_matrix,
    attention_output_matrix,
    bucket_bias_matrix,
    ffn_gain,
    gate_weight,
    up_weight,
    down_projection_weight,
):
    sequences, length, part_width = tokens.shape
    ma_count = lax.axis_size("ma")
    local_heads = bucket_bias_matrix.shape[1]
    inner_width = query_weight.shape[1]
    head_size = inner_width // local_heads
    slab_rows = sequences * length
    token_rows = tokens.reshape(slab_rows, part_width)
    token_float = token_rows.astype(jnp.float32)
    full_weights = (
        lax.all_gather(query_weight, "row", axis=0, tiled=True),
        lax.all_gather(key_weight, "row", axis=0, tiled=True),
        lax.all_gather(value_projection_matrix, "row", axis=0, tiled=True),
    )
    whole_rows, whole_gain = (
        lax.all_gather(token_rows, "ma", axis=1, tiled=True),
        lax.all_gather(attn_gain.reshape(1, part_width), "ma", axis=1, tiled=True),
    )
    normed = rms_scale(whole_rows.astype(jnp.float32), whole_gain[0])
    projected = tuple(
        (jnp.dot(normed, matrix, preferred_element_type=jnp.float32) for matrix in full_weights)
    )
    query_heads, key_heads, value_heads = [
        member.astype(jnp.bfloat16).reshape(sequences, length, local_heads, head_size)
        for member in projected
    ]
    bucket_grid = buckets(length)
    table_rows = jnp.arange(bucket_bias_matrix.shape[0], dtype=jnp.int32)
    bucket_indicator = (table_rows[:, None, None] == bucket_grid[None, :, :]).astype(jnp.float32)
    relative_position_scores = jnp.einsum(
        "dmy,du->umy", bucket_indicator, bucket_bias_matrix, precision=lax.Precision.HIGHEST
    )
    scores = (
        jnp.einsum("sqhd,skhd->shqk", query_heads, key_heads, preferred_element_type=jnp.float32)
        + relative_position_scores[None]
    )
    row_max = jnp.max(scores, axis=-1, keepdims=True)
    exponent = jnp.exp(scores - row_max)
    weights = (exponent / jnp.sum(exponent, axis=-1, keepdims=True)).astype(jnp.bfloat16)
    attended = jnp.einsum(
        "shqk,skhd->sqhd", weights, value_heads, preferred_element_type=jnp.float32
    )
    attended = attended.astype(jnp.bfloat16).reshape(slab_rows, inner_width)
    partial_out = jnp.dot(
        attended,
        lax.all_gather(attention_output_matrix, "row", axis=1, tiled=True),
        preferred_element_type=jnp.float32,
    )
    attn_out = lax.psum_scatter(
        partial_out.astype(jnp.bfloat16), "ma", scatter_dimension=1, tiled=True
    ).astype(jnp.float32)
    residual_stream = (token_float + attn_out).astype(jnp.bfloat16)
    residual_f = residual_stream.astype(jnp.float32)
    norm_gain_vector = ffn_gain.reshape(1, part_width)
    gate_full, up_full, down_full = (gate_weight, up_weight, down_projection_weight)
    group_rows, group_gain = regroup(residual_stream, norm_gain_vector)
    ffn_in = rms_scale(group_rows.astype(jnp.float32), group_gain[0])
    gate_act = jnp.dot(ffn_in, gate_full, preferred_element_type=jnp.float32)
    up_act = jnp.dot(ffn_in, up_full, preferred_element_type=jnp.float32)
    hidden = (jax.nn.gelu(gate_act, approximate=True) * up_act).astype(jnp.bfloat16)
    down_blocks = down_full.reshape(down_full.shape[0], ma_count, part_width)
    down_terms = jnp.einsum("tf,fmd->mtd", hidden, down_blocks, preferred_element_type=jnp.float32)
    down_terms = down_terms.reshape(ma_count * ffn_in.shape[0], part_width)
    ffn_out = lax.psum_scatter(
        down_terms.astype(jnp.bfloat16), ("ma", "row"), scatter_dimension=0, tiled=True
    ).astype(jnp.float32)
    encoded = (residual_f + ffn_out).astype(jnp.bfloat16)
    return encoded.reshape(sequences, length, part_width)


def solution(mesh):
    in_specs = (
        P(("ba", "row"), None, "ma"),
        P("ma"),
        P("row", "ma"),
        P("row", "ma"),
        P("row", "ma"),
        P("ma", "row"),
        P(None, "ma"),
        P("ma"),
        P(None, ("ma", "row")),
        P(None, ("ma", "row")),
        P(("ma", "row"), None),
    )
    out_specs = P(("ba", "row"), None, "ma")
    return jax.shard_map(
        on_device, mesh=mesh, in_specs=in_specs, out_specs=out_specs, check_vma=False
    )
```

profile of v0, /device:TPU:0, one launch (start us, length us, event | category | flops | bytes accessed | tf_op | source)
XLA Modules:
  0.0 752.7 jit_solution(16300057747724244085)
XLA Ops:
  6.5 0.0 copy-start
  6.5 0.0 all-gather.23.cloned.1.call-start
  6.5 0.7 all-gather.23.cloned.1.call-update
  7.3 0.0 all-gather.13.cloned.1.call-start
  7.3 0.7 all-gather.13.cloned.1.call-update
  8.0 0.0 all-gather.15.cloned.1.call-start
  8.1 0.7 all-gather.15.cloned.1.call-update
  8.7 0.0 copy-start.7
  8.8 0.0 all-gather.11.cloned.1.call-start
  8.8 0.5 all-gather.11.cloned.1.call-update
  9.3 0.0 all-gather.17.cloned.1.call-start
  9.4 0.5 all-gather.17.cloned.1.call-update
  9.9 0.0 reduce-scatter.3.cloned.1.call-start
  10.0 0.0 copy-done.7
  10.0 13.7 %all-gather.1 = bf16[4096]{0:T(1024)(128)(2,1)S(1)} all-gather(bf16[1024]{0:T(1024)(128)(2,1)S(1)} %copy-done.7), channel_id=3, replica_groups=mesh['ba'=4,'ma'=4,'row'=2] {'ma'}, dimensions={0}, use_global_device_ids=true | all-gather | bytes 10240 | tf_op jit(solution)/shard_map/all_gather | solution.py:67
  23.7 0.3 fusion.33
  24.1 0.0 copy-done
  24.1 4.2 fusion.7
  28.3 5.3 copy.27
  33.6 23.8 %all-gather.23.cloned.1.call-done = bf16[1,256,4096]{2,1,0:T(8,128)(2,1)} async-done(((bf16[1,256,1024]{2,1,0:T(8,128)(2,1)}), bf16[1,256,4096]{2,1,0:T(8,128)(2,1)}) %all-gather.23.cloned.1.call-update) | async-done | bytes 2097168 | tf_op jit(solution)/shard_map/all_gather | solution.py:66
  57.3 2.1 fusion.8
  59.4 102.2 %all-gather.13.cloned.1.call-done = bf16[4096,1024]{1,0:T(8,128)(2,1)} async-done(((bf16[2048,1024]{1,0:T(8,128)(2,1)}), bf16[4096,1024]{1,0:T(8,128)(2,1)}) %all-gather.13.cloned.1.call-update) | async-done | bytes 8388624 | tf_op jit(solution)/shard_map/all_gather | solution.py:61
  161.7 6.4 convolution_convert_fusion.2
  168.1 0.2 copy.25
  168.3 99.0 %all-gather.15.cloned.1.call-done = bf16[4096,1024]{1,0:T(8,128)(2,1)} async-done(((bf16[2048,1024]{1,0:T(8,128)(2,1)}), bf16[4096,1024]{1,0:T(8,128)(2,1)}) %all-gather.15.cloned.1.call-update) | async-done | bytes 8388624 | tf_op jit(solution)/shard_map/all_gather | solution.py:62
  267.3 0.0 copy-done.6
  267.3 6.6 convolution_convert_fusion.1
  273.9 1.3 copy.26
  275.2 97.5 %all-gather.11.cloned.1.call-done = bf16[4096,1024]{1,0:T(8,128)(2,1)} async-done(((bf16[2048,1024]{1,0:T(8,128)(2,1)}), bf16[4096,1024]{1,0:T(8,128)(2,1)}) %all-gather.11.cloned.1.call-update) | async-done | bytes 8388624 | tf_op jit(solution)/shard_map/all_gather | solution.py:63
  372.7 6.6 convolution_convert_fusion.3
  379.3 1.3 copy.24
  380.6 3.6 bitcast_add_fusion
  384.3 0.0 copy-start.2
  384.3 2.0 copy-done.2
  386.3 0.8 fusion.57
  387.1 5.3 fusion.26
  392.3 85.8 %all-gather.17.cloned.1.call-done = bf16[1024,4096]{1,0:T(8,128)(2,1)} async-done(((bf16[1024,2048]{1,0:T(8,128)(2,1)}), bf16[1024,4096]{1,0:T(8,128)(2,1)}) %all-gather.17.cloned.1.call-update) | async-done | bytes 8388624 | tf_op jit(solution)/shard_map/all_gather | solution.py:96
  478.1 7.2 convolution_convert_fusion
  485.3 0.0 reduce-scatter.3.cloned.1.call-update
  485.4 0.0 all-gather.19.cloned.1.call-start
  485.4 43.7 %reduce-scatter.3.cloned.1.call-done = bf16[256,1024]{1,0:T(8,128)(2,1)} async-done(((bf16[256,4096]{1,0:T(8,128)(2,1)}), bf16[256,1024]{1,0:T(8,128)(2,1)}) %reduce-scatter.3.cloned.1.call-update) | async-done | bytes 524304 | tf_op jit(solution)/shard_map/reduce_scatter | solution.py:99
  529.1 0.0 copy-done.5
  529.1 2.0 fusion.30
  531.2 0.0 all-gather.19.cloned.1.call-update
  531.2 0.0 all-gather.21.cloned.1.call-start
  531.2 45.0 %all-gather.19.cloned.1.call-done = bf16[256,4096]{1,0:T(8,128)(2,1)} async-done(((bf16[256,1024]{1,0:T(8,128)(2,1)}), bf16[256,4096]{1,0:T(8,128)(2,1)}) %all-gather.19.cloned.1.call-update) | async-done | bytes 2097168 | tf_op jit(solution)/shard_map/all_gather | solution.py:32
  576.2 0.0 all-gather.21.cloned.1.call-update
  576.2 0.0 reduce-scatter.5.cloned.1.call-start
  576.3 0.0 copy-done.8
  576.3 12.2 %all-gather.2 = bf16[4096]{0:T(1024)(128)(2,1)S(1)} all-gather(bf16[1024]{0:T(1024)(128)(2,1)S(1)} %copy-done.8), channel_id=4, replica_groups=mesh['ba'=4,'ma'=4,'row'=2] {'ma'}, dimensions={0}, use_global_device_ids=true | all-gather | bytes 10240 | tf_op jit(solution)/shard_map/all_gather | solution.py:33
  588.5 44.9 %all-gather.21.cloned.1.call-done = bf16[512,4096]{1,0:T(8,128)(2,1)} async-done(((bf16[256,4096]{1,0:T(8,128)(2,1)}), bf16[512,4096]{1,0:T(8,128)(2,1)}) %all-gather.21.cloned.1.call-update) | async-done | bytes 4194320 | tf_op jit(solution)/shard_map/all_gather | solution.py:35
  633.3 3.2 fusion.1
  636.6 0.2 copy-done.4
  636.8 7.7 %fusion.28 = f32[512,1024]{1,0:T(8,128)S(1)} fusion(bf16[4096,1024]{1,0:T(8,128)(2,1)} %param.19, bf16[512,4096]{1,0:T(8,128)(2,1)S(1)} %copy-done.4, f32[4096]{0:T(1024)S(1)} %mul.97, f32[512]{0:T(512)S(1)} %add_rsqrt_fusion), kind=kOutput, calls=%fused_computation.38 | convolution fusion | flops 4303355904 | bytes 14698496 | tf_op jit(solution)/shard_map/dot_general | solution.py:108
  644.5 0.0 slice-done
  644.5 0.0 slice-done.1
  644.6 4.9 fusion.25
  649.4 0.0 slice-done.2
  649.4 0.0 slice-done.3
  649.5 0.0 copy-start.1
  649.5 6.2 fusion.12
  655.6 0.0 reduce-scatter.5.cloned.1.call-update
  655.6 88.5 %reduce-scatter.5.cloned.1.call-done = bf16[256,1024]{1,0:T(8,128)(2,1)} async-done(((bf16[2048,1024]{1,0:T(8,128)(2,1)}), bf16[256,1024]{1,0:T(8,128)(2,1)}) %reduce-scatter.5.cloned.1.call-update) | async-done | bytes 524304 | tf_op jit(solution)/shard_map/reduce_scatter | solution.py:114
  744.1 2.0 fusion.31
  (17 shorter events, 0.0 us)
Async XLA Ops:
  6.5 17.5 %copy-start = (f32[32,16]{0,1:T(8,128)S(1)}, f32[32,16]{0,1:T(8,128)}, u32[]{:S(2)}) copy-start(f32[32,16]{0,1:T(8,128)} %param.17) | copy-start | bytes 6148
  6.5 50.8 %all-gather.23.cloned.1.call-start = ((), (), s32[]{:S(2)}) async-start(), calls=%async_computation.10 | async-start | bytes 2621440 | tf_op jit(solution)/shard_map/all_gather | solution.py:66
  7.3 154.4 %all-gather.13.cloned.1.call-start = ((), (), s32[]{:S(2)}) async-start(), calls=%async_computation.3 | async-start | bytes 12582912 | tf_op jit(solution)/shard_map/all_gather | solution.py:61
  8.0 259.3 %all-gather.15.cloned.1.call-start = ((), (), s32[]{:S(2)}) async-start(), calls=%async_computation.4 | async-start | bytes 12582912 | tf_op jit(solution)/shard_map/all_gather | solution.py:62
  8.7 1.2 copy-start.7
  8.8 363.9 %all-gather.11.cloned.1.call-start = ((), (), s32[]{:S(2)}) async-start(), calls=%async_computation.2 | async-start | bytes 12582912 | tf_op jit(solution)/shard_map/all_gather | solution.py:63
  9.3 468.8 %all-gather.17.cloned.1.call-start = ((), (), s32[]{:S(2)}) async-start(), calls=%async_computation.5 | async-start | bytes 12582912 | tf_op jit(solution)/shard_map/all_gather | solution.py:96
  9.9 519.2 %reduce-scatter.3.cloned.1.call-start = ((), (), s32[]{:S(2)}) async-start(), calls=%async_computation.6 | async-start | bytes 2621440 | tf_op jit(solution)/shard_map/reduce_scatter | solution.py:99
  59.4 207.9 %copy-start.6 = (bf16[1,256,4096]{2,1,0:T(8,128)(2,1)S(1)}, bf16[1,256,4096]{2,1,0:T(8,128)(2,1)}, u32[]{:S(2)}) copy-start(bf16[1,256,4096]{2,1,0:T(8,128)(2,1)} %all-gather.23.cloned.1.call-done) | copy-start | bytes 6291460
  384.3 2.1 copy-start.2
  478.1 51.0 %copy-start.5 = (bf16[1,256,1024]{2,1,0:T(8,128)(2,1)S(1)}, bf16[1,256,1024]{2,1,0:T(8,128)(2,1)}, u32[]{:S(2)}) copy-start(bf16[1,256,1024]{2,1,0:T(8,128)(2,1)} %param.11) | copy-start | bytes 1572868
  485.3 91.0 %copy-start.8 = (bf16[1024]{0:T(1024)(128)(2,1)S(1)}, bf16[1024]{0:T(1024)(128)(2,1)}, u32[]{:S(2)}) copy-start(bf16[1024]{0:T(1024)(128)(2,1)} %param.18) | copy-start | bytes 6148
  485.4 90.9 %all-gather.19.cloned.1.call-start = ((), (), s32[]{:S(2)}) async-start(), calls=%async_computation.7 | async-start | bytes 2621440 | tf_op jit(solution)/shard_map/all_gather | solution.py:32
  531.2 102.1 %all-gather.21.cloned.1.call-start = ((), (), s32[]{:S(2)}) async-start(), calls=%async_computation.8 | async-start | bytes 6291456 | tf_op jit(solution)/shard_map/all_gather | solution.py:35
  576.2 167.9 %reduce-scatter.5.cloned.1.call-start = ((), (), s32[]{:S(2)}) async-start(), calls=%async_computation.9 | async-start | bytes 4718592 | tf_op jit(solution)/shard_map/reduce_scatter | solution.py:114
  633.3 3.4 copy-start.4
  633.3 11.2 %slice-start = ((s8[8388608]{0:T(1024)(128)(4,1)}), s8[4194304]{0:T(1024)(128)(4,1)S(1)}, s32[]{:S(2)}) async-start(s8[8388608]{0:T(1024)(128)(4,1)} %bitcast.54), calls=%async_computation.11 | async-start | bytes 8388608
  633.3 16.1 %slice-start.2 = ((s8[8388608]{0:T(1024)(128)(4,1)}), s8[4194304]{0:T(1024)(128)(4,1)S(1)}, s32[]{:S(2)}) async-start(s8[8388608]{0:T(1024)(128)(4,1)} %bitcast.56), calls=%async_computation.13 | async-start | bytes 8388608
  636.8 7.8 %slice-start.1 = ((s8[8388608]{0:T(1024)(128)(4,1)}), s8[4194304]{0:T(1024)(128)(4,1)S(1)}, s32[]{:S(2)}) async-start(s8[8388608]{0:T(1024)(128)(4,1)} %bitcast.54), calls=%async_computation.12 | async-start | bytes 8388608
  636.8 12.7 %slice-start.3 = ((s8[8388608]{0:T(1024)(128)(4,1)}), s8[4194304]{0:T(1024)(128)(4,1)S(1)}, s32[]{:S(2)}) async-start(s8[8388608]{0:T(1024)(128)(4,1)} %bitcast.56), calls=%async_computation.14 | async-start | bytes 8388608
  649.5 96.7 %copy-start.1 = (f32[32,16]{0,1:T(8,128)S(1)}, f32[32,16]{0,1:T(8,128)}, u32[]{:S(2)}) copy-start(f32[32,16]{0,1:T(8,128)} %param.17) | copy-start | bytes 6148
  655.6 88.5 %copy-start.3 = (bf16[256,1024]{1,0:T(8,128)(2,1)S(1)}, bf16[256,1024]{1,0:T(8,128)(2,1)}, u32[]{:S(2)}) copy-start(bf16[256,1024]{1,0:T(8,128)(2,1)} %fusion.30) | copy-start | bytes 1572868
Sparse Core Ops, SparseCore 0:
  8.9 48.3 all-gather.22
  58.9 102.7 all-gather.12
  163.2 104.0 all-gather.14
  268.7 103.9 all-gather.10
  374.1 103.9 all-gather.16
  485.5 43.6 reduce-scatter.2
  531.3 44.8 all-gather.18
  577.8 55.5 all-gather.20
  655.8 88.3 reduce-scatter.4
where the time goes:
time: 753 us
  waiting for transfers between devices  634 us (84%)
  matrix products  58.6 us (8%)
  blocking collectives  25.9 us (3%)
  between operations  13.4 us (2%)
  other arithmetic  10.5 us (1%)
  local copies, waits for them, and re-layouts  10.4 us (1%)
    all_gather x1, waiting for transfers between devices, on_device(): lax.all_gather(query_weight, 'row', axis=0, tiled=True)  102 us
    all_gather x1, waiting for transfers between devices, on_device(): lax.all_gather(key_weight, 'row', axis=0, tiled=True)  99 us
    all_gather x1, waiting for transfers between devices, on_device(): lax.all_gather(value_projection_matrix, 'row', axis=0, tiled=True)  97.5 us
    reduce_scatter x1, waiting for transfers between devices, on_device(): lax.psum_scatter(down_terms.astype(jnp.bfloat16), ('ma', 'row'), scatter_...  88.5 us
    all_gather x1, waiting for transfers between devices, on_device(): lax.all_gather(attention_output_matrix, 'row', axis=1, tiled=True)  85.8 us
    all_gather x1, waiting for transfers between devices, regroup(): lax.all_gather(values, 'ma', axis=1, tiled=True)  45 us
    all_gather x1, waiting for transfers between devices, regroup(): stacked = lax.all_gather(widened[0], 'row', axis=0, tiled=True)  44.9 us
    reduce_scatter x1, waiting for transfers between devices, on_device(): lax.psum_scatter(partial_out.astype(jnp.bfloat16), 'ma', scatter_dimensio...  43.7 us
  transfers between devices with their start and end apart: 9, of which 9 were waited for; matrix products, arithmetic and copies ran while one was open for 6% of the time, Pallas kernels for 0%

commit v1 on v0

--- a/solution.py
+++ b/solution.py
@@ -5,6 +5,18 @@
 
 bucket_thresholds = (1, 2, 3, 4, 5, 6, 7, 8, 11, 16, 23, 32, 45, 64, 91, 128)
 epsilon = 1e-06
+
+
+def doubled_up(value, axis, dim):
+    ways, here = (lax.axis_size(axis), lax.axis_index(axis))
+    grown, reach = (value, 1)
+    while reach < ways:
+        theirs = lax.ppermute(grown, axis, [(d, d ^ reach) for d in range(ways)])
+        mine_first = jnp.concatenate([grown, theirs], axis=dim)
+        theirs_first = jnp.concatenate([theirs, grown], axis=dim)
+        grown = jnp.where(here & reach == 0, mine_first, theirs_first)
+        reach = 2 * reach
+    return grown
 
 
 def buckets(length):
@@ -92,9 +104,7 @@
     )
     attended = attended.astype(jnp.bfloat16).reshape(slab_rows, inner_width)
     partial_out = jnp.dot(
-        attended,
-        lax.all_gather(attention_output_matrix, "row", axis=1, tiled=True),
-        preferred_element_type=jnp.float32,
+        attended, doubled_up(attention_output_matrix, "row", 1), preferred_element_type=jnp.float32
     )
     attn_out = lax.psum_scatter(
         partial_out.astype(jnp.bfloat16), "ma", scatter_dimension=1, tiled=True

time: 753 us -> 704 us (0.935)
  waiting for transfers between devices: 634 us -> 580 us
    all_gather x1 -> x0, waiting for transfers between devices: 85.8 us -> none  [on_device(): lax.all_gather(attention_output_matrix, 'row', axis=1, tiled=True)]
    all_gather x1, waiting for transfers between devices: 102 us -> 134 us  [on_device(): lax.all_gather(query_weight, 'row', axis=0, tiled=True)]
  transfers between devices with their start and end apart: 9 -> 9, of which waited for: 9 -> 8; matrix products, arithmetic and copies ran while one was open for 6% -> 6% of each run, Pallas kernels for 0% -> 0%
where the time goes in v1:
time: 704 us; the launch traced here: 703 us
  waiting for transfers between devices  580 us (82%)
  matrix products  61.9 us (9%)
  blocking collectives  24.2 us (3%)
  between operations  13.7 us (2%)
  other arithmetic  10.5 us (1%)
  local copies, waits for them, and re-layouts  10.2 us (1%)
    all_gather x1, waiting for transfers between devices, on_device(): lax.all_gather(query_weight, 'row', axis=0, tiled=True)  134 us
    all_gather x1, waiting for transfers between devices, on_device(): lax.all_gather(key_weight, 'row', axis=0, tiled=True)  100 us
    all_gather x1, waiting for transfers between devices, on_device(): lax.all_gather(value_projection_matrix, 'row', axis=0, tiled=True)  97.5 us
    reduce_scatter x1, waiting for transfers between devices, on_device(): lax.psum_scatter(down_terms.astype(jnp.bfloat16), ('ma', 'row'), scatter_...  88.5 us
    all_gather x1, waiting for transfers between devices, regroup(): stacked = lax.all_gather(widened[0], 'row', axis=0, tiled=True)  45.1 us
    all_gather x1, waiting for transfers between devices, regroup(): lax.all_gather(values, 'ma', axis=1, tiled=True)  45 us
    reduce_scatter x1, waiting for transfers between devices, on_device(): lax.psum_scatter(partial_out.astype(jnp.bfloat16), 'ma', scatter_dimensio...  43.7 us
    all_gather x1, waiting for transfers between devices, on_device(): lax.all_gather(token_rows, 'ma', axis=1, tiled=True)  22.9 us
  transfers between devices with their start and end apart: 9, of which 8 were waited for; matrix products, arithmetic and copies ran while one was open for 6% of the time, Pallas kernels for 0%

profile of v1, /device:TPU:0, one launch (start us, length us, event | category | flops | bytes accessed | tf_op | source)
XLA Modules:
  0.0 703.4 jit_solution(3059858825615201934)
XLA Ops:
  6.5 0.0 copy-start
  6.5 0.0 all-gather.20.cloned.1.call-start
  6.5 0.7 all-gather.20.cloned.1.call-update
  7.3 0.0 all-gather.12.cloned.1.call-start
  7.3 0.7 all-gather.12.cloned.1.call-update
  8.0 0.0 copy-start.7
  8.0 0.0 all-gather.14.cloned.1.call-start
  8.1 0.7 all-gather.14.cloned.1.call-update
  8.8 0.0 all-gather.10.cloned.1.call-start
  8.8 0.5 all-gather.10.cloned.1.call-update
  9.3 0.0 reduce-scatter.3.cloned.1.call-start
  9.4 3.1 collective-permute-start
  12.4 0.0 copy-done.7
  12.4 12.3 %all-gather.1 = bf16[4096]{0:T(1024)(128)(2,1)S(1)} all-gather(bf16[1024]{0:T(1024)(128)(2,1)S(1)} %copy-done.7), channel_id=3, replica_groups=mesh['ba'=4,'ma'=4,'row'=2] {'ma'}, dimensions={0}, use_global_device_ids=true | all-gather | bytes 10240 | tf_op jit(solution)/shard_map/all_gather | solution.py:79
  24.7 0.3 fusion.41
  25.1 0.0 copy-done
  25.1 4.1 fusion.13
  29.2 5.2 copy.27
  34.4 22.9 %all-gather.20.cloned.1.call-done = bf16[1,256,4096]{2,1,0:T(8,128)(2,1)} async-done(((bf16[1,256,1024]{2,1,0:T(8,128)(2,1)}), bf16[1,256,4096]{2,1,0:T(8,128)(2,1)}) %all-gather.20.cloned.1.call-update) | async-done | bytes 2097168 | tf_op jit(solution)/shard_map/all_gather | solution.py:78
  57.3 2.1 fusion.16
  59.4 133.9 %all-gather.12.cloned.1.call-done = bf16[4096,1024]{1,0:T(8,128)(2,1)} async-done(((bf16[2048,1024]{1,0:T(8,128)(2,1)}), bf16[4096,1024]{1,0:T(8,128)(2,1)}) %all-gather.12.cloned.1.call-update) | async-done | bytes 8388624 | tf_op jit(solution)/shard_map/all_gather | solution.py:73
  193.4 6.4 convolution_convert_fusion.1
  199.8 0.2 copy.25
  200.0 100.4 %all-gather.14.cloned.1.call-done = bf16[4096,1024]{1,0:T(8,128)(2,1)} async-done(((bf16[2048,1024]{1,0:T(8,128)(2,1)}), bf16[4096,1024]{1,0:T(8,128)(2,1)}) %all-gather.14.cloned.1.call-update) | async-done | bytes 8388624 | tf_op jit(solution)/shard_map/all_gather | solution.py:74
  300.4 0.0 copy-done.6
  300.4 6.6 convolution_convert_fusion
  307.0 1.3 copy.26
  308.3 97.5 %all-gather.10.cloned.1.call-done = bf16[4096,1024]{1,0:T(8,128)(2,1)} async-done(((bf16[2048,1024]{1,0:T(8,128)(2,1)}), bf16[4096,1024]{1,0:T(8,128)(2,1)}) %all-gather.10.cloned.1.call-update) | async-done | bytes 8388624 | tf_op jit(solution)/shard_map/all_gather | solution.py:75
  405.8 6.6 convolution_convert_fusion.2
  412.4 1.2 copy.24
  413.6 3.0 bitcast_add_fusion
  416.6 0.0 copy-start.2
  416.6 1.9 copy-done.2
  418.5 0.8 fusion.66
  419.3 4.5 fusion.34
  423.8 0.0 collective-permute-done
  423.8 0.0 copy-start.5
  423.9 11.9 %fusion.15 = bf16[256,4096]{1,0:T(8,128)(2,1)} fusion(bf16[256,1024]{0,1:T(8,128)(2,1)S(1)} %bitcast.57, bf16[1024,2048]{1,0:T(8,128)(2,1)} %collective-permute-done, bf16[1024,2048]{1,0:T(8,128)(2,1)} %param.16, pred[]{:T(512)S(6)} %eq.19), kind=kOutput, calls=%fused_computation.21 | convolution fusion | flops 2186280960 | bytes 11010049 | tf_op jit(solution)/shard_map/dot_general | solution.py:106
  435.7 0.0 reduce-scatter.3.cloned.1.call-update
  435.8 0.0 all-gather.16.cloned.1.call-start
  435.8 43.7 %reduce-scatter.3.cloned.1.call-done = bf16[256,1024]{1,0:T(8,128)(2,1)} async-done(((bf16[256,4096]{1,0:T(8,128)(2,1)}), bf16[256,1024]{1,0:T(8,128)(2,1)}) %reduce-scatter.3.cloned.1.call-update) | async-done | bytes 524304 | tf_op jit(solution)/shard_map/reduce_scatter | solution.py:109
  479.5 0.0 copy-done.5
  479.5 2.0 fusion.38
  481.6 0.0 all-gather.16.cloned.1.call-update
  481.6 0.0 all-gather.18.cloned.1.call-start
  481.6 45.0 %all-gather.16.cloned.1.call-done = bf16[256,4096]{1,0:T(8,128)(2,1)} async-done(((bf16[256,1024]{1,0:T(8,128)(2,1)}), bf16[256,4096]{1,0:T(8,128)(2,1)}) %all-gather.16.cloned.1.call-update) | async-done | bytes 2097168 | tf_op jit(solution)/shard_map/all_gather | solution.py:44
  526.6 0.0 all-gather.18.cloned.1.call-update
  526.6 0.0 reduce-scatter.5.cloned.1.call-start
  526.7 0.0 copy-done.8
  526.7 11.9 %all-gather.2 = bf16[4096]{0:T(1024)(128)(2,1)S(1)} all-gather(bf16[1024]{0:T(1024)(128)(2,1)S(1)} %copy-done.8), channel_id=4, replica_groups=mesh['ba'=4,'ma'=4,'row'=2] {'ma'}, dimensions={0}, use_global_device_ids=true | all-gather | bytes 10240 | tf_op jit(solution)/shard_map/all_gather | solution.py:45
  538.6 45.1 %all-gather.18.cloned.1.call-done = bf16[512,4096]{1,0:T(8,128)(2,1)} async-done(((bf16[256,4096]{1,0:T(8,128)(2,1)}), bf16[512,4096]{1,0:T(8,128)(2,1)}) %all-gather.18.cloned.1.call-update) | async-done | bytes 4194320 | tf_op jit(solution)/shard_map/all_gather | solution.py:47
  583.7 3.2 fusion.1
  587.0 0.2 copy-done.4
  587.2 7.7 %fusion.36 = f32[512,1024]{1,0:T(8,128)S(1)} fusion(bf16[4096,1024]{1,0:T(8,128)(2,1)} %param.19, bf16[512,4096]{1,0:T(8,128)(2,1)S(1)} %copy-done.4, f32[4096]{0:T(1024)S(1)} %mul.97, f32[512]{0:T(512)S(1)} %add_rsqrt_fusion), kind=kOutput, calls=%fused_computation.46 | convolution fusion | flops 4303355904 | bytes 14698496 | tf_op jit(solution)/shard_map/dot_general | solution.py:118
  594.9 0.0 slice-done
  594.9 0.0 slice-done.1
  595.0 4.9 fusion.33
  599.9 0.0 copy-start.1
  599.9 6.1 fusion.20
  606.0 0.0 reduce-scatter.5.cloned.1.call-update
  606.1 88.5 %reduce-scatter.5.cloned.1.call-done = bf16[256,1024]{1,0:T(8,128)(2,1)} async-done(((bf16[2048,1024]{1,0:T(8,128)(2,1)}), bf16[256,1024]{1,0:T(8,128)(2,1)}) %reduce-scatter.5.cloned.1.call-update) | async-done | bytes 524304 | tf_op jit(solution)/shard_map/reduce_scatter | solution.py:124
  694.5 0.0 copy-done.3
  694.5 2.0 fusion.39
  696.5 0.0 copy-done.1
  (16 shorter events, 0.0 us)
Async XLA Ops:
  6.5 18.5 %copy-start = (f32[32,16]{0,1:T(8,128)S(1)}, f32[32,16]{0,1:T(8,128)}, u32[]{:S(2)}) copy-start(f32[32,16]{0,1:T(8,128)} %param.17) | copy-start | bytes 6148
  6.5 50.8 %all-gather.20.cloned.1.call-start = ((), (), s32[]{:S(2)}) async-start(), calls=%async_computation.9 | async-start | bytes 2621440 | tf_op jit(solution)/shard_map/all_gather | solution.py:78
  7.3 186.1 %all-gather.12.cloned.1.call-start = ((), (), s32[]{:S(2)}) async-start(), calls=%async_computation.3 | async-start | bytes 12582912 | tf_op jit(solution)/shard_map/all_gather | solution.py:73
  8.0 4.4 copy-start.7
  8.0 292.4 %all-gather.14.cloned.1.call-start = ((), (), s32[]{:S(2)}) async-start(), calls=%async_computation.4 | async-start | bytes 12582912 | tf_op jit(solution)/shard_map/all_gather | solution.py:74
  8.8 397.0 %all-gather.10.cloned.1.call-start = ((), (), s32[]{:S(2)}) async-start(), calls=%async_computation.2 | async-start | bytes 12582912 | tf_op jit(solution)/shard_map/all_gather | solution.py:75
  9.3 470.2 %reduce-scatter.3.cloned.1.call-start = ((), (), s32[]{:S(2)}) async-start(), calls=%async_computation.5 | async-start | bytes 2621440 | tf_op jit(solution)/shard_map/reduce_scatter | solution.py:109
  9.4 414.5 %collective-permute-start = (bf16[1024,2048]{1,0:T(8,128)(2,1)}, bf16[1024,2048]{1,0:T(8,128)(2,1)}, u32[]{:S(2)}, u32[]{:S(2)}) collective-permute-start(bf16[1024,2048]{1,0:T(8,128)(2,1)} %param.16), channel_id=1, source_target_pairs={{0,1},{1,0},{2,3},{3,2},{4,5},{5,4},{6,7},{7,6},{8,9},{9,8},{10,11... | collective-permute-start | bytes 12582920 | tf_op jit(solution)/shard_map/ppermute | solution.py:14
  59.4 241.0 %copy-start.6 = (bf16[1,256,4096]{2,1,0:T(8,128)(2,1)S(1)}, bf16[1,256,4096]{2,1,0:T(8,128)(2,1)}, u32[]{:S(2)}) copy-start(bf16[1,256,4096]{2,1,0:T(8,128)(2,1)} %all-gather.20.cloned.1.call-done) | copy-start | bytes 6291460
  416.6 1.9 copy-start.2
  423.8 55.7 %copy-start.5 = (bf16[1,256,1024]{2,1,0:T(8,128)(2,1)S(1)}, bf16[1,256,1024]{2,1,0:T(8,128)(2,1)}, u32[]{:S(2)}) copy-start(bf16[1,256,1024]{2,1,0:T(8,128)(2,1)} %param.11) | copy-start | bytes 1572868
  435.7 91.0 %copy-start.8 = (bf16[1024]{0:T(1024)(128)(2,1)S(1)}, bf16[1024]{0:T(1024)(128)(2,1)}, u32[]{:S(2)}) copy-start(bf16[1024]{0:T(1024)(128)(2,1)} %param.18) | copy-start | bytes 6148
  435.8 90.9 %all-gather.16.cloned.1.call-start = ((), (), s32[]{:S(2)}) async-start(), calls=%async_computation.6 | async-start | bytes 2621440 | tf_op jit(solution)/shard_map/all_gather | solution.py:44
  481.6 102.1 %all-gather.18.cloned.1.call-start = ((), (), s32[]{:S(2)}) async-start(), calls=%async_computation.7 | async-start | bytes 6291456 | tf_op jit(solution)/shard_map/all_gather | solution.py:47
  526.6 167.9 %reduce-scatter.5.cloned.1.call-start = ((), (), s32[]{:S(2)}) async-start(), calls=%async_computation.8 | async-start | bytes 4718592 | tf_op jit(solution)/shard_map/reduce_scatter | solution.py:124
  583.7 3.4 copy-start.4
  583.7 11.2 %slice-start = ((s8[8388608]{0:T(1024)(128)(4,1)}), s8[4194304]{0:T(1024)(128)(4,1)S(1)}, s32[]{:S(2)}) async-start(s8[8388608]{0:T(1024)(128)(4,1)} %bitcast.52), calls=%async_computation.10 | async-start | bytes 8388608
  583.7 16.1 %slice-start.2 = ((s8[8388608]{0:T(1024)(128)(4,1)}), s8[4194304]{0:T(1024)(128)(4,1)S(1)}, s32[]{:S(2)}) async-start(s8[8388608]{0:T(1024)(128)(4,1)} %bitcast.54), calls=%async_computation.12 | async-start | bytes 8388608
  587.2 7.8 %slice-start.1 = ((s8[8388608]{0:T(1024)(128)(4,1)}), s8[4194304]{0:T(1024)(128)(4,1)S(1)}, s32[]{:S(2)}) async-start(s8[8388608]{0:T(1024)(128)(4,1)} %bitcast.52), calls=%async_computation.11 | async-start | bytes 8388608
  587.2 12.7 %slice-start.3 = ((s8[8388608]{0:T(1024)(128)(4,1)}), s8[4194304]{0:T(1024)(128)(4,1)S(1)}, s32[]{:S(2)}) async-start(s8[8388608]{0:T(1024)(128)(4,1)} %bitcast.54), calls=%async_computation.13 | async-start | bytes 8388608
  599.9 96.7 %copy-start.1 = (f32[32,16]{0,1:T(8,128)S(1)}, f32[32,16]{0,1:T(8,128)}, u32[]{:S(2)}) copy-start(f32[32,16]{0,1:T(8,128)} %param.17) | copy-start | bytes 6148
  606.0 88.5 %copy-start.3 = (bf16[256,1024]{1,0:T(8,128)(2,1)S(1)}, bf16[256,1024]{1,0:T(8,128)(2,1)}, u32[]{:S(2)}) copy-start(bf16[256,1024]{1,0:T(8,128)(2,1)} %fusion.38) | copy-start | bytes 1572868
Sparse Core Ops, SparseCore 0:
  8.9 48.3 all-gather.19
  58.9 134.4 all-gather.11
  194.9 105.4 all-gather.13
  301.8 103.9 all-gather.9
  435.9 43.5 reduce-scatter.2
  481.7 44.8 all-gather.15
  528.2 55.5 all-gather.17
  606.2 88.2 reduce-scatter.4
